TPU v7x, 32 devices: a whole 2x2x4 slice. The times are simulated.
32 devices in a mesh: grp: 2 (over y), row: 16 (over z, x, core).
Axes of the slice: x: 2, y: 2, z: 4, core: 2. Of those that a mesh axis runs over, the one named last changes fastest.
Arguments:
- diag_blocks: float32 [8192, 512], P('row'), may hold values from -0.6 to 2.6
- lower_coupling: float32 [8192, 64], P('row'), may hold values from -0.3125 to 0.3125
- upper_coupling: float32 [8192, 64], P('row'), may hold values from -0.3125 to 0.3125
- right_sides: float32 [8192, 1024], P('row', 'grp'), parts along dimension 1, may hold values from -108 to 108
Outputs:
- solution: float32 [8192, 1024], P('row', 'grp'), parts along dimension 1
- res_norms: float32 [8, 1024], P(None, 'grp'), parts along dimension 1
There are 2 independent parts, one for each index of `grp`. A program takes and returns all parts, laid end to end along the dimension named above; an argument that names none is the same for every part. Nothing has to cross between parts.
All inputs are finite; a program needn't handle non-finite values.
Results may differ from a plain program's by a relative error of at most 0.0001.
Values sent between devices are 32-bit elements; how exact they have to be, the bound alone decides.
A program may use at most 64 MiB of HBM per device.

v0:
```python
import jax
import jax.numpy as jnp
from jax import lax
from jax.sharding import PartitionSpec as P

SWEEPS = 8


def extended(shard, sides, width):
    for axis, dim in sides:
        size, length = (lax.axis_size(axis), shard.shape[dim])
        up = [(i, (i + 1) % size) for i in range(size - 1)]
        down = [(j, i) for i, j in up]
        last = lax.slice_in_dim(shard, length - width, length, axis=dim)
        first = lax.slice_in_dim(shard, 0, width, axis=dim)
        before = lax.ppermute(last, axis, up)
        after = lax.ppermute(first, axis, down)
        shard = jnp.concatenate([before, shard, after], axis=dim)
    return shard


def matmul(left, right):
    return jnp.dot(left, right, precision=lax.Precision.HIGHEST, preferred_element_type=jnp.float32)


def local(diag_blocks, lower_coupling, upper_coupling, right_sides):
    pivots = jnp.diagonal(diag_blocks)[:, None]
    width = lower_coupling.shape[1]
    solution = jnp.zeros_like(right_sides)
    partials = []
    for sweep_index in range(SWEEPS):
        padded = extended(solution, (("row", 0),), width)
        before = padded[:width]
        after = padded[padded.shape[0] - width :]
        images = (
            matmul(diag_blocks, solution)
            + matmul(lower_coupling, before)
            + matmul(upper_coupling, after)
        )
        residual = right_sides - images
        local_sums = jnp.sum(residual * residual, axis=0)
        solution = solution + residual / pivots
        partials.append(local_sums)
    res_norms = jnp.sqrt(lax.psum(jnp.stack(partials), "row"))
    return (solution, res_norms)


def solution(mesh):
    return jax.shard_map(
        local,
        mesh=mesh,
        in_specs=(P("row", None), P("row", None), P("row", None), P("row", "grp")),
        out_specs=(P("row", "grp"), P(None, "grp")),
        check_vma=False,
    )
```

profile of v0, /device:TPU:0, one launch (start us, length us, event | category | flops | bytes accessed | tf_op | source)
XLA Modules:
  0.0 163.6 jit_solution(15000186278195526279)
XLA Ops:
  0.7 1.4 collective-permute-start.1
  2.1 3.0 %collective-permute-start = (f32[64,512]{1,0:T(8,128)S(1)}, f32[64,512]{1,0:T(8,128)S(1)}, u32[]{:S(2)}, u32[]{:S(2)}) collective-permute-start(f32[64,512]{1,0:T(8,128)S(1)} %broadcast.16), channel_id=1, source_target_pairs={{0,1},{1,2},{2,3},{3,4},{4,5},{5,6},{6,7},{7,8},{8,9},{9,10},{10,1... | collective-permute-start | bytes 393224 | tf_op jit(solution)/shard_map/ppermute | solution.py:16
  5.2 8.5 %gather_fusion = f32[512]{0:T(512)S(1)} fusion(f32[512,512]{1,0:T(8,128)} %param.4, s32[512]{0:T(512)S(1)} %bitcast.87), kind=kCustom, calls=%fused_computation | custom fusion | bytes 8192 | tf_op jit(solution)/shard_map/jit(diagonal)/cond/branch_0_fun/gather | solution.py:27
  13.8 1.0 fusion.24
  14.9 1.2 multiply_reduce_fusion.7
  16.1 4.5 %collective-permute-start.2 = (f32[64,512]{1,0:T(8,128)S(1)}, f32[64,512]{1,0:T(8,128)S(1)}, u32[]{:S(2)}, u32[]{:S(2)}) collective-permute-start(f32[64,512]{1,0:T(8,128)S(1)} %get-tuple-element.31), channel_id=1, source_target_pairs={{0,1},{1,2},{2,3},{3,4},{4,5},{5,6},{6,7},{7,8},{8,9},{9,10},{10,1... | collective-permute-start | bytes 393224 | tf_op jit(solution)/shard_map/ppermute | solution.py:16
  20.6 1.9 %fusion.25 = f32[512,512]{0,1:T(8,128)S(1)} fusion(f32[512,512]{1,0:T(8,128)S(1)} %get-tuple-element.17, f32[512,512]{1,0:T(8,128)S(1)} %copy-done.1), kind=kOutput, calls=%fused_computation.59 | convolution fusion | flops 1610612736 | bytes 3145728 | tf_op jit(solution)/shard_map/dot_general | solution.py:23
  22.5 1.3 collective-permute-start.3
  23.8 1.0 convolution_add_fusion.13
  24.9 0.9 collective-permute-done.3
  25.8 1.2 multiply_reduce_fusion.6
  27.0 5.7 %collective-permute-start.4 = (f32[64,512]{1,0:T(8,128)S(1)}, f32[64,512]{1,0:T(8,128)S(1)}, u32[]{:S(2)}, u32[]{:S(2)}) collective-permute-start(f32[64,512]{1,0:T(8,128)S(1)} %get-tuple-element.29), channel_id=1, source_target_pairs={{0,1},{1,2},{2,3},{3,4},{4,5},{5,6},{6,7},{7,8},{8,9},{9,10},{10,1... | collective-permute-start | bytes 393224 | tf_op jit(solution)/shard_map/ppermute | solution.py:16
  32.7 1.9 %fusion.26 = f32[512,512]{0,1:T(8,128)S(1)} fusion(f32[512,512]{1,0:T(8,128)S(1)} %get-tuple-element.15, f32[512,512]{1,0:T(8,128)S(1)} %copy-done.1), kind=kOutput, calls=%fused_computation.60 | convolution fusion | flops 1610612736 | bytes 3145728 | tf_op jit(solution)/shard_map/dot_general | solution.py:23
  34.6 1.3 collective-permute-start.5
  35.9 1.0 convolution_add_fusion.11
  36.9 0.9 collective-permute-done.5
  37.8 1.2 multiply_reduce_fusion.5
  39.0 6.0 %collective-permute-start.6 = (f32[64,512]{1,0:T(8,128)S(1)}, f32[64,512]{1,0:T(8,128)S(1)}, u32[]{:S(2)}, u32[]{:S(2)}) collective-permute-start(f32[64,512]{1,0:T(8,128)S(1)} %get-tuple-element.27), channel_id=1, source_target_pairs={{0,1},{1,2},{2,3},{3,4},{4,5},{5,6},{6,7},{7,8},{8,9},{9,10},{10,1... | collective-permute-start | bytes 393224 | tf_op jit(solution)/shard_map/ppermute | solution.py:16
  45.1 1.9 %fusion.27 = f32[512,512]{0,1:T(8,128)S(1)} fusion(f32[512,512]{1,0:T(8,128)S(1)} %get-tuple-element.13, f32[512,512]{1,0:T(8,128)S(1)} %copy-done.1), kind=kOutput, calls=%fused_computation.61 | convolution fusion | flops 1610612736 | bytes 3145728 | tf_op jit(solution)/shard_map/dot_general | solution.py:23
  47.0 1.3 collective-permute-start.7
  48.3 1.0 convolution_add_fusion.9
  49.3 0.9 collective-permute-done.7
  50.2 1.2 multiply_reduce_fusion.4
  51.4 5.9 %collective-permute-start.8 = (f32[64,512]{1,0:T(8,128)S(1)}, f32[64,512]{1,0:T(8,128)S(1)}, u32[]{:S(2)}, u32[]{:S(2)}) collective-permute-start(f32[64,512]{1,0:T(8,128)S(1)} %get-tuple-element.25), channel_id=1, source_target_pairs={{0,1},{1,2},{2,3},{3,4},{4,5},{5,6},{6,7},{7,8},{8,9},{9,10},{10,1... | collective-permute-start | bytes 393224 | tf_op jit(solution)/shard_map/ppermute | solution.py:16
  57.3 1.9 %fusion.28 = f32[512,512]{0,1:T(8,128)S(1)} fusion(f32[512,512]{1,0:T(8,128)S(1)} %get-tuple-element.11, f32[512,512]{1,0:T(8,128)S(1)} %copy-done.1), kind=kOutput, calls=%fused_computation.62 | convolution fusion | flops 1610612736 | bytes 3145728 | tf_op jit(solution)/shard_map/dot_general | solution.py:23
  59.2 1.3 collective-permute-start.9
  60.5 1.0 convolution_add_fusion.7
  61.5 0.9 collective-permute-done.9
  62.4 1.2 multiply_reduce_fusion.3
  63.6 5.9 %collective-permute-start.10 = (f32[64,512]{1,0:T(8,128)S(1)}, f32[64,512]{1,0:T(8,128)S(1)}, u32[]{:S(2)}, u32[]{:S(2)}) collective-permute-start(f32[64,512]{1,0:T(8,128)S(1)} %get-tuple-element.23), channel_id=1, source_target_pairs={{0,1},{1,2},{2,3},{3,4},{4,5},{5,6},{6,7},{7,8},{8,9},{9,10},{10,1... | collective-permute-start | bytes 393224 | tf_op jit(solution)/shard_map/ppermute | solution.py:16
  69.5 1.9 %fusion.29 = f32[512,512]{0,1:T(8,128)S(1)} fusion(f32[512,512]{1,0:T(8,128)S(1)} %get-tuple-element.9, f32[512,512]{1,0:T(8,128)S(1)} %copy-done.1), kind=kOutput, calls=%fused_computation.63 | convolution fusion | flops 1610612736 | bytes 3145728 | tf_op jit(solution)/shard_map/dot_general | solution.py:23
  71.4 1.3 collective-permute-start.11
  72.7 1.0 convolution_add_fusion.5
  73.7 0.9 collective-permute-done.11
  74.6 1.2 multiply_reduce_fusion.2
  75.9 6.1 %collective-permute-start.12 = (f32[64,512]{1,0:T(8,128)S(1)}, f32[64,512]{1,0:T(8,128)S(1)}, u32[]{:S(2)}, u32[]{:S(2)}) collective-permute-start(f32[64,512]{1,0:T(8,128)S(1)} %get-tuple-element.21), channel_id=1, source_target_pairs={{0,1},{1,2},{2,3},{3,4},{4,5},{5,6},{6,7},{7,8},{8,9},{9,10},{10,1... | collective-permute-start | bytes 393224 | tf_op jit(solution)/shard_map/ppermute | solution.py:16
  82.0 1.9 %fusion.30 = f32[512,512]{0,1:T(8,128)S(1)} fusion(f32[512,512]{1,0:T(8,128)S(1)} %get-tuple-element.7, f32[512,512]{1,0:T(8,128)S(1)} %copy-done.1), kind=kOutput, calls=%fused_computation.64 | convolution fusion | flops 1610612736 | bytes 3145728 | tf_op jit(solution)/shard_map/dot_general | solution.py:23
  83.8 1.3 collective-permute-start.13
  85.1 1.0 convolution_add_fusion.3
  86.2 0.9 collective-permute-done.13
  87.1 1.2 multiply_reduce_fusion.1
  88.3 5.9 %collective-permute-start.14 = (f32[64,512]{1,0:T(8,128)S(1)}, f32[64,512]{1,0:T(8,128)S(1)}, u32[]{:S(2)}, u32[]{:S(2)}) collective-permute-start(f32[64,512]{1,0:T(8,128)S(1)} %get-tuple-element.19), channel_id=1, source_target_pairs={{0,1},{1,2},{2,3},{3,4},{4,5},{5,6},{6,7},{7,8},{8,9},{9,10},{10,1... | collective-permute-start | bytes 393224 | tf_op jit(solution)/shard_map/ppermute | solution.py:16
  94.2 1.9 %fusion.31 = f32[512,512]{0,1:T(8,128)S(1)} fusion(f32[512,512]{1,0:T(8,128)S(1)} %get-tuple-element.5, f32[512,512]{1,0:T(8,128)S(1)} %copy-done.1), kind=kOutput, calls=%fused_computation.65 | convolution fusion | flops 1610612736 | bytes 3145728 | tf_op jit(solution)/shard_map/dot_general | solution.py:23
  96.1 1.3 collective-permute-start.15
  97.4 1.0 convolution_add_fusion.1
  98.4 0.9 collective-permute-done.15
  99.3 2.2 %multiply_reduce_fusion = (f32[512]{0:T(512)S(1)}, f32[512,512]{1,0:T(8,128)}) fusion(f32[512,512]{1,0:T(8,128)S(1)} %get-tuple-element.5, f32[512]{0:T(512)S(1)} %gather_fusion, f32[512,512]{1,0:T(8,128)S(1)} %copy-done.3, f32[512,512]{0,1:T(8,128)S(1)} %convolution_add_fusion.1, f32[64,512]{1,0:T(8,128)S(1)} %collective-permute-done.15, ...), kind=kOutput, calls=%fused_computation.33 | convolution fusion | flops 202898944 | bytes 4460544 | tf_op jit(solution)/shard_map/dot_general | solution.py:23
  101.5 61.5 %psum.7 = f32[8,512]{1,0:T(8,128)S(1)} all-reduce(f32[8,512]{1,0:T(8,128)S(1)} %stack.35), channel_id=1, replica_groups=mesh['grp'=2,'row'=16] {'row'}, use_global_device_ids=true, to_apply=%region_9.10 | all-reduce | flops 4096 | bytes 32768 | tf_op jit(solution)/shard_map/psum | solution.py:44
  (29 shorter events, 1.0 us)
Async XLA Ops:
  0.6 13.2 %copy-start = (f32[512,64]{0,1:T(8,128)S(1)}, f32[512,64]{0,1:T(8,128)}, u32[]{:S(2)}) copy-start(f32[512,64]{0,1:T(8,128)} %param.6) | copy-start | bytes 393220
  0.7 13.2 %collective-permute-start.1 = (f32[64,512]{1,0:T(8,128)S(1)}, f32[64,512]{1,0:T(8,128)S(1)}, u32[]{:S(2)}, u32[]{:S(2)}) collective-permute-start(f32[64,512]{1,0:T(8,128)S(1)} %broadcast.16), channel_id=1, source_target_pairs={{1,0},{2,1},{3,2},{4,3},{5,4},{6,5},{7,6},{8,7},{9,8},{10,9},{11,1... | collective-permute-start | bytes 393224 | tf_op jit(solution)/shard_map/ppermute | solution.py:17
  2.1 12.8 %collective-permute-start = (f32[64,512]{1,0:T(8,128)S(1)}, f32[64,512]{1,0:T(8,128)S(1)}, u32[]{:S(2)}, u32[]{:S(2)}) collective-permute-start(f32[64,512]{1,0:T(8,128)S(1)} %broadcast.16), channel_id=1, source_target_pairs={{0,1},{1,2},{2,3},{3,4},{4,5},{5,6},{6,7},{7,8},{8,9},{9,10},{10,1... | collective-permute-start | bytes 393224 | tf_op jit(solution)/shard_map/ppermute | solution.py:16
  5.2 8.5 %copy-start.1 = (f32[512,512]{1,0:T(8,128)S(1)}, f32[512,512]{1,0:T(8,128)}, u32[]{:S(2)}) copy-start(f32[512,512]{1,0:T(8,128)} %param.4) | copy-start | bytes 3145732
  13.6 1.2 copy-start.3
  13.8 1.1 copy-start.2
  16.1 7.7 %collective-permute-start.2 = (f32[64,512]{1,0:T(8,128)S(1)}, f32[64,512]{1,0:T(8,128)S(1)}, u32[]{:S(2)}, u32[]{:S(2)}) collective-permute-start(f32[64,512]{1,0:T(8,128)S(1)} %get-tuple-element.31), channel_id=1, source_target_pairs={{0,1},{1,2},{2,3},{3,4},{4,5},{5,6},{6,7},{7,8},{8,9},{9,10},{10,1... | collective-permute-start | bytes 393224 | tf_op jit(solution)/shard_map/ppermute | solution.py:16
  22.5 3.2 %collective-permute-start.3 = (f32[64,512]{1,0:T(8,128)S(1)}, f32[64,512]{1,0:T(8,128)S(1)}, u32[]{:S(2)}, u32[]{:S(2)}) collective-permute-start(f32[64,512]{1,0:T(8,128)S(1)} %get-tuple-element.30), channel_id=1, source_target_pairs={{1,0},{2,1},{3,2},{4,3},{5,4},{6,5},{7,6},{8,7},{9,8},{10,9},{11,1... | collective-permute-start | bytes 393224 | tf_op jit(solution)/shard_map/ppermute | solution.py:17
  27.0 8.9 %collective-permute-start.4 = (f32[64,512]{1,0:T(8,128)S(1)}, f32[64,512]{1,0:T(8,128)S(1)}, u32[]{:S(2)}, u32[]{:S(2)}) collective-permute-start(f32[64,512]{1,0:T(8,128)S(1)} %get-tuple-element.29), channel_id=1, source_target_pairs={{0,1},{1,2},{2,3},{3,4},{4,5},{5,6},{6,7},{7,8},{8,9},{9,10},{10,1... | collective-permute-start | bytes 393224 | tf_op jit(solution)/shard_map/ppermute | solution.py:16
  34.6 3.2 %collective-permute-start.5 = (f32[64,512]{1,0:T(8,128)S(1)}, f32[64,512]{1,0:T(8,128)S(1)}, u32[]{:S(2)}, u32[]{:S(2)}) collective-permute-start(f32[64,512]{1,0:T(8,128)S(1)} %get-tuple-element.28), channel_id=1, source_target_pairs={{1,0},{2,1},{3,2},{4,3},{5,4},{6,5},{7,6},{8,7},{9,8},{10,9},{11,1... | collective-permute-start | bytes 393224 | tf_op jit(solution)/shard_map/ppermute | solution.py:17
  39.0 9.2 %collective-permute-start.6 = (f32[64,512]{1,0:T(8,128)S(1)}, f32[64,512]{1,0:T(8,128)S(1)}, u32[]{:S(2)}, u32[]{:S(2)}) collective-permute-start(f32[64,512]{1,0:T(8,128)S(1)} %get-tuple-element.27), channel_id=1, source_target_pairs={{0,1},{1,2},{2,3},{3,4},{4,5},{5,6},{6,7},{7,8},{8,9},{9,10},{10,1... | collective-permute-start | bytes 393224 | tf_op jit(solution)/shard_map/ppermute | solution.py:16
  47.0 3.2 %collective-permute-start.7 = (f32[64,512]{1,0:T(8,128)S(1)}, f32[64,512]{1,0:T(8,128)S(1)}, u32[]{:S(2)}, u32[]{:S(2)}) collective-permute-start(f32[64,512]{1,0:T(8,128)S(1)} %get-tuple-element.26), channel_id=1, source_target_pairs={{1,0},{2,1},{3,2},{4,3},{5,4},{6,5},{7,6},{8,7},{9,8},{10,9},{11,1... | collective-permute-start | bytes 393224 | tf_op jit(solution)/shard_map/ppermute | solution.py:17
  51.4 9.1 %collective-permute-start.8 = (f32[64,512]{1,0:T(8,128)S(1)}, f32[64,512]{1,0:T(8,128)S(1)}, u32[]{:S(2)}, u32[]{:S(2)}) collective-permute-start(f32[64,512]{1,0:T(8,128)S(1)} %get-tuple-element.25), channel_id=1, source_target_pairs={{0,1},{1,2},{2,3},{3,4},{4,5},{5,6},{6,7},{7,8},{8,9},{9,10},{10,1... | collective-permute-start | bytes 393224 | tf_op jit(solution)/shard_map/ppermute | solution.py:16
  59.2 3.2 %collective-permute-start.9 = (f32[64,512]{1,0:T(8,128)S(1)}, f32[64,512]{1,0:T(8,128)S(1)}, u32[]{:S(2)}, u32[]{:S(2)}) collective-permute-start(f32[64,512]{1,0:T(8,128)S(1)} %get-tuple-element.24), channel_id=1, source_target_pairs={{1,0},{2,1},{3,2},{4,3},{5,4},{6,5},{7,6},{8,7},{9,8},{10,9},{11,1... | collective-permute-start | bytes 393224 | tf_op jit(solution)/shard_map/ppermute | solution.py:17
  63.6 9.1 %collective-permute-start.10 = (f32[64,512]{1,0:T(8,128)S(1)}, f32[64,512]{1,0:T(8,128)S(1)}, u32[]{:S(2)}, u32[]{:S(2)}) collective-permute-start(f32[64,512]{1,0:T(8,128)S(1)} %get-tuple-element.23), channel_id=1, source_target_pairs={{0,1},{1,2},{2,3},{3,4},{4,5},{5,6},{6,7},{7,8},{8,9},{9,10},{10,1... | collective-permute-start | bytes 393224 | tf_op jit(solution)/shard_map/ppermute | solution.py:16
  71.4 3.2 %collective-permute-start.11 = (f32[64,512]{1,0:T(8,128)S(1)}, f32[64,512]{1,0:T(8,128)S(1)}, u32[]{:S(2)}, u32[]{:S(2)}) collective-permute-start(f32[64,512]{1,0:T(8,128)S(1)} %get-tuple-element.22), channel_id=1, source_target_pairs={{1,0},{2,1},{3,2},{4,3},{5,4},{6,5},{7,6},{8,7},{9,8},{10,9},{11,1... | collective-permute-start | bytes 393224 | tf_op jit(solution)/shard_map/ppermute | solution.py:17
  75.9 9.3 %collective-permute-start.12 = (f32[64,512]{1,0:T(8,128)S(1)}, f32[64,512]{1,0:T(8,128)S(1)}, u32[]{:S(2)}, u32[]{:S(2)}) collective-permute-start(f32[64,512]{1,0:T(8,128)S(1)} %get-tuple-element.21), channel_id=1, source_target_pairs={{0,1},{1,2},{2,3},{3,4},{4,5},{5,6},{6,7},{7,8},{8,9},{9,10},{10,1... | collective-permute-start | bytes 393224 | tf_op jit(solution)/shard_map/ppermute | solution.py:16
  83.8 3.2 %collective-permute-start.13 = (f32[64,512]{1,0:T(8,128)S(1)}, f32[64,512]{1,0:T(8,128)S(1)}, u32[]{:S(2)}, u32[]{:S(2)}) collective-permute-start(f32[64,512]{1,0:T(8,128)S(1)} %get-tuple-element.20), channel_id=1, source_target_pairs={{1,0},{2,1},{3,2},{4,3},{5,4},{6,5},{7,6},{8,7},{9,8},{10,9},{11,1... | collective-permute-start | bytes 393224 | tf_op jit(solution)/shard_map/ppermute | solution.py:17
  88.3 9.1 %collective-permute-start.14 = (f32[64,512]{1,0:T(8,128)S(1)}, f32[64,512]{1,0:T(8,128)S(1)}, u32[]{:S(2)}, u32[]{:S(2)}) collective-permute-start(f32[64,512]{1,0:T(8,128)S(1)} %get-tuple-element.19), channel_id=1, source_target_pairs={{0,1},{1,2},{2,3},{3,4},{4,5},{5,6},{6,7},{7,8},{8,9},{9,10},{10,1... | collective-permute-start | bytes 393224 | tf_op jit(solution)/shard_map/ppermute | solution.py:16
  96.1 3.2 %collective-permute-start.15 = (f32[64,512]{1,0:T(8,128)S(1)}, f32[64,512]{1,0:T(8,128)S(1)}, u32[]{:S(2)}, u32[]{:S(2)}) collective-permute-start(f32[64,512]{1,0:T(8,128)S(1)} %get-tuple-element.18), channel_id=1, source_target_pairs={{1,0},{2,1},{3,2},{4,3},{5,4},{6,5},{7,6},{8,7},{9,8},{10,9},{11,1... | collective-permute-start | bytes 393224 | tf_op jit(solution)/shard_map/ppermute | solution.py:17
where the time goes:
time: 164 us
  blocking collectives  61.5 us (38%)
  starting transfers between devices  53.4 us (33%)
  matrix products  31.8 us (19%)
  local copies, waits for them, and re-layouts  9.29 us (6%)
  waiting for transfers between devices  6.33 us (4%)
    psum x1, blocking collectives, local(): res_norms = jnp.sqrt(lax.psum(jnp.stack(partials), 'row'))  61.5 us
    ppermute x8, starting transfers between devices, extended(): before = lax.ppermute(last, axis, up)  42.9 us
    dot_general x23, matrix products, matmul(): jnp.dot(left, right, precision=lax.Precision.HIGHEST, preferred_element_t...  31.8 us
    ppermute x8, starting transfers between devices, extended(): after = lax.ppermute(first, axis, down)  10.5 us
    gather x1, local copies, waits for them, and re-layouts, local(): pivots = jnp.diagonal(diag_blocks)[:, None]  8.46 us
    ppermute x8, waiting for transfers between devices, extended(): after = lax.ppermute(first, axis, down)  6.31 us
  transfers between devices with their start and end apart: 16, of which 7 were waited for; matrix products, arithmetic and copies ran while one was open for 18% of the time, Pallas kernels for 0%

commit v1 on v0

--- a/solution.py
+++ b/solution.py
@@ -2,8 +2,10 @@
 import jax.numpy as jnp
 from jax import lax
 from jax.sharding import PartitionSpec as P
+from jax.lax import all_gather
 
 SWEEPS = 8
+set_part = lambda here_x: jnp.sum(all_gather(here_x, "row"), 0)
 
 
 def extended(shard, sides, width):
@@ -41,7 +43,7 @@
         local_sums = jnp.sum(residual * residual, axis=0)
         solution = solution + residual / pivots
         partials.append(local_sums)
-    res_norms = jnp.sqrt(lax.psum(jnp.stack(partials), "row"))
+    res_norms = jnp.sqrt(set_part(jnp.stack(partials)))
     return (solution, res_norms)
 
 

time: 164 us -> 125 us (0.76)
  blocking collectives: 61.5 us -> 22 us
    psum x1 -> x0, blocking collectives: 61.5 us -> none  [local(): res_norms = jnp.sqrt(lax.psum(jnp.stack(partials), 'row'))]
    all_gather x0 -> x1, blocking collectives: none -> 22 us  [set_part = lambda here_x: jnp.sum(all_gather(here_x, 'row'), 0)]
  transfers between devices with their start and end apart: 16 -> 16, of which waited for: 7 -> 7; matrix products, arithmetic and copies ran while one was open for 18% -> 24% of each run, Pallas kernels for 0% -> 0%
where the time goes in v1:
time: 125 us; the launch traced here: 124 us
  starting transfers between devices  53.4 us (43%)
  matrix products  31.8 us (25%)
  blocking collectives  22 us (18%)
  local copies, waits for them, and re-layouts  9.29 us (7%)
  waiting for transfers between devices  6.33 us (5%)
    ppermute x8, starting transfers between devices, extended(): before = lax.ppermute(last, axis, up)  42.9 us
    dot_general x23, matrix products, matmul(): jnp.dot(left, right, precision=lax.Precision.HIGHEST, preferred_element_t...  31.8 us
    all_gather x1, blocking collectives, set_part = lambda here_x: jnp.sum(all_gather(here_x, 'row'), 0)  22 us
    ppermute x8, starting transfers between devices, extended(): after = lax.ppermute(first, axis, down)  10.5 us
    gather x1, local copies, waits for them, and re-layouts, local(): pivots = jnp.diagonal(diag_blocks)[:, None]  8.46 us
    ppermute x8, waiting for transfers between devices, extended(): after = lax.ppermute(first, axis, down)  6.31 us
  transfers between devices with their start and end apart: 16, of which 7 were waited for; matrix products, arithmetic and copies ran while one was open for 24% of the time, Pallas kernels for 0%

profile of v1, /device:TPU:0, one launch (start us, length us, event | category | flops | bytes accessed | tf_op | source)
XLA Modules:
  0.0 124.1 jit_solution(14763441105539395630)
XLA Ops:
  0.7 1.4 %collective-permute-start.1 = (f32[64,512]{1,0:T(8,128)S(1)}, f32[64,512]{1,0:T(8,128)S(1)}, u32[]{:S(2)}, u32[]{:S(2)}) collective-permute-start(f32[64,512]{1,0:T(8,128)S(1)} %broadcast.16), channel_id=1, source_target_pairs={{1,0},{2,1},{3,2},{4,3},{5,4},{6,5},{7,6},{8,7},{9,8},{10,9},{11,1... | collective-permute-start | bytes 393224 | tf_op jit(solution)/shard_map/ppermute | solution.py:19
  2.1 3.0 %collective-permute-start = (f32[64,512]{1,0:T(8,128)S(1)}, f32[64,512]{1,0:T(8,128)S(1)}, u32[]{:S(2)}, u32[]{:S(2)}) collective-permute-start(f32[64,512]{1,0:T(8,128)S(1)} %broadcast.16), channel_id=1, source_target_pairs={{0,1},{1,2},{2,3},{3,4},{4,5},{5,6},{6,7},{7,8},{8,9},{9,10},{10,1... | collective-permute-start | bytes 393224 | tf_op jit(solution)/shard_map/ppermute | solution.py:18
  5.2 8.5 %gather_fusion = f32[512]{0:T(512)S(1)} fusion(f32[512,512]{1,0:T(8,128)} %param.4, s32[512]{0:T(512)S(1)} %bitcast.89), kind=kCustom, calls=%fused_computation | custom fusion | bytes 8192 | tf_op jit(solution)/shard_map/jit(diagonal)/cond/branch_0_fun/gather | solution.py:29
  13.8 1.0 fusion.24
  14.9 1.2 multiply_reduce_fusion.7
  16.1 4.5 %collective-permute-start.2 = (f32[64,512]{1,0:T(8,128)S(1)}, f32[64,512]{1,0:T(8,128)S(1)}, u32[]{:S(2)}, u32[]{:S(2)}) collective-permute-start(f32[64,512]{1,0:T(8,128)S(1)} %get-tuple-element.31), channel_id=1, source_target_pairs={{0,1},{1,2},{2,3},{3,4},{4,5},{5,6},{6,7},{7,8},{8,9},{9,10},{10,1... | collective-permute-start | bytes 393224 | tf_op jit(solution)/shard_map/ppermute | solution.py:18
  20.6 1.9 %fusion.25 = f32[512,512]{0,1:T(8,128)S(1)} fusion(f32[512,512]{1,0:T(8,128)S(1)} %get-tuple-element.17, f32[512,512]{1,0:T(8,128)S(1)} %copy-done.1), kind=kOutput, calls=%fused_computation.60 | convolution fusion | flops 1610612736 | bytes 3145728 | tf_op jit(solution)/shard_map/dot_general | solution.py:25
  22.5 1.3 %collective-permute-start.3 = (f32[64,512]{1,0:T(8,128)S(1)}, f32[64,512]{1,0:T(8,128)S(1)}, u32[]{:S(2)}, u32[]{:S(2)}) collective-permute-start(f32[64,512]{1,0:T(8,128)S(1)} %get-tuple-element.30), channel_id=1, source_target_pairs={{1,0},{2,1},{3,2},{4,3},{5,4},{6,5},{7,6},{8,7},{9,8},{10,9},{11,1... | collective-permute-start | bytes 393224 | tf_op jit(solution)/shard_map/ppermute | solution.py:19
  23.8 1.0 convolution_add_fusion.13
  24.9 0.9 collective-permute-done.3
  25.8 1.2 multiply_reduce_fusion.6
  27.0 5.7 %collective-permute-start.4 = (f32[64,512]{1,0:T(8,128)S(1)}, f32[64,512]{1,0:T(8,128)S(1)}, u32[]{:S(2)}, u32[]{:S(2)}) collective-permute-start(f32[64,512]{1,0:T(8,128)S(1)} %get-tuple-element.29), channel_id=1, source_target_pairs={{0,1},{1,2},{2,3},{3,4},{4,5},{5,6},{6,7},{7,8},{8,9},{9,10},{10,1... | collective-permute-start | bytes 393224 | tf_op jit(solution)/shard_map/ppermute | solution.py:18
  32.7 1.9 %fusion.26 = f32[512,512]{0,1:T(8,128)S(1)} fusion(f32[512,512]{1,0:T(8,128)S(1)} %get-tuple-element.15, f32[512,512]{1,0:T(8,128)S(1)} %copy-done.1), kind=kOutput, calls=%fused_computation.61 | convolution fusion | flops 1610612736 | bytes 3145728 | tf_op jit(solution)/shard_map/dot_general | solution.py:25
  34.6 1.3 %collective-permute-start.5 = (f32[64,512]{1,0:T(8,128)S(1)}, f32[64,512]{1,0:T(8,128)S(1)}, u32[]{:S(2)}, u32[]{:S(2)}) collective-permute-start(f32[64,512]{1,0:T(8,128)S(1)} %get-tuple-element.28), channel_id=1, source_target_pairs={{1,0},{2,1},{3,2},{4,3},{5,4},{6,5},{7,6},{8,7},{9,8},{10,9},{11,1... | collective-permute-start | bytes 393224 | tf_op jit(solution)/shard_map/ppermute | solution.py:19
  35.9 1.0 convolution_add_fusion.11
  36.9 0.9 collective-permute-done.5
  37.8 1.2 multiply_reduce_fusion.5
  39.0 6.0 %collective-permute-start.6 = (f32[64,512]{1,0:T(8,128)S(1)}, f32[64,512]{1,0:T(8,128)S(1)}, u32[]{:S(2)}, u32[]{:S(2)}) collective-permute-start(f32[64,512]{1,0:T(8,128)S(1)} %get-tuple-element.27), channel_id=1, source_target_pairs={{0,1},{1,2},{2,3},{3,4},{4,5},{5,6},{6,7},{7,8},{8,9},{9,10},{10,1... | collective-permute-start | bytes 393224 | tf_op jit(solution)/shard_map/ppermute | solution.py:18
  45.1 1.9 %fusion.27 = f32[512,512]{0,1:T(8,128)S(1)} fusion(f32[512,512]{1,0:T(8,128)S(1)} %get-tuple-element.13, f32[512,512]{1,0:T(8,128)S(1)} %copy-done.1), kind=kOutput, calls=%fused_computation.62 | convolution fusion | flops 1610612736 | bytes 3145728 | tf_op jit(solution)/shard_map/dot_general | solution.py:25
  47.0 1.3 %collective-permute-start.7 = (f32[64,512]{1,0:T(8,128)S(1)}, f32[64,512]{1,0:T(8,128)S(1)}, u32[]{:S(2)}, u32[]{:S(2)}) collective-permute-start(f32[64,512]{1,0:T(8,128)S(1)} %get-tuple-element.26), channel_id=1, source_target_pairs={{1,0},{2,1},{3,2},{4,3},{5,4},{6,5},{7,6},{8,7},{9,8},{10,9},{11,1... | collective-permute-start | bytes 393224 | tf_op jit(solution)/shard_map/ppermute | solution.py:19
  48.3 1.0 convolution_add_fusion.9
  49.3 0.9 collective-permute-done.7
  50.2 1.2 multiply_reduce_fusion.4
  51.4 5.9 %collective-permute-start.8 = (f32[64,512]{1,0:T(8,128)S(1)}, f32[64,512]{1,0:T(8,128)S(1)}, u32[]{:S(2)}, u32[]{:S(2)}) collective-permute-start(f32[64,512]{1,0:T(8,128)S(1)} %get-tuple-element.25), channel_id=1, source_target_pairs={{0,1},{1,2},{2,3},{3,4},{4,5},{5,6},{6,7},{7,8},{8,9},{9,10},{10,1... | collective-permute-start | bytes 393224 | tf_op jit(solution)/shard_map/ppermute | solution.py:18
  57.3 1.9 %fusion.28 = f32[512,512]{0,1:T(8,128)S(1)} fusion(f32[512,512]{1,0:T(8,128)S(1)} %get-tuple-element.11, f32[512,512]{1,0:T(8,128)S(1)} %copy-done.1), kind=kOutput, calls=%fused_computation.63 | convolution fusion | flops 1610612736 | bytes 3145728 | tf_op jit(solution)/shard_map/dot_general | solution.py:25
  59.2 1.3 %collective-permute-start.9 = (f32[64,512]{1,0:T(8,128)S(1)}, f32[64,512]{1,0:T(8,128)S(1)}, u32[]{:S(2)}, u32[]{:S(2)}) collective-permute-start(f32[64,512]{1,0:T(8,128)S(1)} %get-tuple-element.24), channel_id=1, source_target_pairs={{1,0},{2,1},{3,2},{4,3},{5,4},{6,5},{7,6},{8,7},{9,8},{10,9},{11,1... | collective-permute-start | bytes 393224 | tf_op jit(solution)/shard_map/ppermute | solution.py:19
  60.5 1.0 convolution_add_fusion.7
  61.5 0.9 collective-permute-done.9
  62.4 1.2 multiply_reduce_fusion.3
  63.6 5.9 %collective-permute-start.10 = (f32[64,512]{1,0:T(8,128)S(1)}, f32[64,512]{1,0:T(8,128)S(1)}, u32[]{:S(2)}, u32[]{:S(2)}) collective-permute-start(f32[64,512]{1,0:T(8,128)S(1)} %get-tuple-element.23), channel_id=1, source_target_pairs={{0,1},{1,2},{2,3},{3,4},{4,5},{5,6},{6,7},{7,8},{8,9},{9,10},{10,1... | collective-permute-start | bytes 393224 | tf_op jit(solution)/shard_map/ppermute | solution.py:18
  69.5 1.9 %fusion.29 = f32[512,512]{0,1:T(8,128)S(1)} fusion(f32[512,512]{1,0:T(8,128)S(1)} %get-tuple-element.9, f32[512,512]{1,0:T(8,128)S(1)} %copy-done.1), kind=kOutput, calls=%fused_computation.64 | convolution fusion | flops 1610612736 | bytes 3145728 | tf_op jit(solution)/shard_map/dot_general | solution.py:25
  71.4 1.3 %collective-permute-start.11 = (f32[64,512]{1,0:T(8,128)S(1)}, f32[64,512]{1,0:T(8,128)S(1)}, u32[]{:S(2)}, u32[]{:S(2)}) collective-permute-start(f32[64,512]{1,0:T(8,128)S(1)} %get-tuple-element.22), channel_id=1, source_target_pairs={{1,0},{2,1},{3,2},{4,3},{5,4},{6,5},{7,6},{8,7},{9,8},{10,9},{11,1... | collective-permute-start | bytes 393224 | tf_op jit(solution)/shard_map/ppermute | solution.py:19
  72.7 1.0 convolution_add_fusion.5
  73.7 0.9 collective-permute-done.11
  74.6 1.2 multiply_reduce_fusion.2
  75.9 6.1 %collective-permute-start.12 = (f32[64,512]{1,0:T(8,128)S(1)}, f32[64,512]{1,0:T(8,128)S(1)}, u32[]{:S(2)}, u32[]{:S(2)}) collective-permute-start(f32[64,512]{1,0:T(8,128)S(1)} %get-tuple-element.21), channel_id=1, source_target_pairs={{0,1},{1,2},{2,3},{3,4},{4,5},{5,6},{6,7},{7,8},{8,9},{9,10},{10,1... | collective-permute-start | bytes 393224 | tf_op jit(solution)/shard_map/ppermute | solution.py:18
  82.0 1.9 %fusion.30 = f32[512,512]{0,1:T(8,128)S(1)} fusion(f32[512,512]{1,0:T(8,128)S(1)} %get-tuple-element.7, f32[512,512]{1,0:T(8,128)S(1)} %copy-done.1), kind=kOutput, calls=%fused_computation.65 | convolution fusion | flops 1610612736 | bytes 3145728 | tf_op jit(solution)/shard_map/dot_general | solution.py:25
  83.8 1.3 %collective-permute-start.13 = (f32[64,512]{1,0:T(8,128)S(1)}, f32[64,512]{1,0:T(8,128)S(1)}, u32[]{:S(2)}, u32[]{:S(2)}) collective-permute-start(f32[64,512]{1,0:T(8,128)S(1)} %get-tuple-element.20), channel_id=1, source_target_pairs={{1,0},{2,1},{3,2},{4,3},{5,4},{6,5},{7,6},{8,7},{9,8},{10,9},{11,1... | collective-permute-start | bytes 393224 | tf_op jit(solution)/shard_map/ppermute | solution.py:19
  85.1 1.0 convolution_add_fusion.3
  86.2 0.9 collective-permute-done.13
  87.1 1.2 multiply_reduce_fusion.1
  88.3 5.9 %collective-permute-start.14 = (f32[64,512]{1,0:T(8,128)S(1)}, f32[64,512]{1,0:T(8,128)S(1)}, u32[]{:S(2)}, u32[]{:S(2)}) collective-permute-start(f32[64,512]{1,0:T(8,128)S(1)} %get-tuple-element.19), channel_id=1, source_target_pairs={{0,1},{1,2},{2,3},{3,4},{4,5},{5,6},{6,7},{7,8},{8,9},{9,10},{10,1... | collective-permute-start | bytes 393224 | tf_op jit(solution)/shard_map/ppermute | solution.py:18
  94.2 1.9 %fusion.31 = f32[512,512]{0,1:T(8,128)S(1)} fusion(f32[512,512]{1,0:T(8,128)S(1)} %get-tuple-element.5, f32[512,512]{1,0:T(8,128)S(1)} %copy-done.1), kind=kOutput, calls=%fused_computation.66 | convolution fusion | flops 1610612736 | bytes 3145728 | tf_op jit(solution)/shard_map/dot_general | solution.py:25
  96.1 1.3 %collective-permute-start.15 = (f32[64,512]{1,0:T(8,128)S(1)}, f32[64,512]{1,0:T(8,128)S(1)}, u32[]{:S(2)}, u32[]{:S(2)}) collective-permute-start(f32[64,512]{1,0:T(8,128)S(1)} %get-tuple-element.18), channel_id=1, source_target_pairs={{1,0},{2,1},{3,2},{4,3},{5,4},{6,5},{7,6},{8,7},{9,8},{10,9},{11,1... | collective-permute-start | bytes 393224 | tf_op jit(solution)/shard_map/ppermute | solution.py:19
  97.4 1.0 convolution_add_fusion.1
  98.4 0.9 collective-permute-done.15
  99.3 2.2 %multiply_reduce_fusion = (f32[512]{0:T(512)S(1)}, f32[512,512]{1,0:T(8,128)}) fusion(f32[512,512]{1,0:T(8,128)S(1)} %get-tuple-element.5, f32[512]{0:T(512)S(1)} %gather_fusion, f32[512,512]{1,0:T(8,128)S(1)} %copy-done.3, f32[512,512]{0,1:T(8,128)S(1)} %convolution_add_fusion.1, f32[64,512]{1,0:T(8,128)S(1)} %collective-permute-done.15, ...), kind=kOutput, calls=%fused_computation.33 | convolution fusion | flops 202898944 | bytes 4460544 | tf_op jit(solution)/shard_map/dot_general | solution.py:25
  101.5 22.0 %all-gather = f32[128,512]{1,0:T(8,128)S(1)} all-gather(f32[8,512]{1,0:T(8,128)S(1)} %stack.35), channel_id=2, replica_groups=mesh['grp'=2,'row'=16] {'row'}, dimensions={0}, use_global_device_ids=true | all-gather | bytes 278528 | tf_op jit(solution)/shard_map/all_gather | solution.py:8
  (30 shorter events, 1.0 us)
Async XLA Ops:
  0.6 13.2 %copy-start = (f32[512,64]{0,1:T(8,128)S(1)}, f32[512,64]{0,1:T(8,128)}, u32[]{:S(2)}) copy-start(f32[512,64]{0,1:T(8,128)} %param.6) | copy-start | bytes 393220
  0.7 13.2 %collective-permute-start.1 = (f32[64,512]{1,0:T(8,128)S(1)}, f32[64,512]{1,0:T(8,128)S(1)}, u32[]{:S(2)}, u32[]{:S(2)}) collective-permute-start(f32[64,512]{1,0:T(8,128)S(1)} %broadcast.16), channel_id=1, source_target_pairs={{1,0},{2,1},{3,2},{4,3},{5,4},{6,5},{7,6},{8,7},{9,8},{10,9},{11,1... | collective-permute-start | bytes 393224 | tf_op jit(solution)/shard_map/ppermute | solution.py:19
  2.1 12.8 %collective-permute-start = (f32[64,512]{1,0:T(8,128)S(1)}, f32[64,512]{1,0:T(8,128)S(1)}, u32[]{:S(2)}, u32[]{:S(2)}) collective-permute-start(f32[64,512]{1,0:T(8,128)S(1)} %broadcast.16), channel_id=1, source_target_pairs={{0,1},{1,2},{2,3},{3,4},{4,5},{5,6},{6,7},{7,8},{8,9},{9,10},{10,1... | collective-permute-start | bytes 393224 | tf_op jit(solution)/shard_map/ppermute | solution.py:18
  5.2 8.5 %copy-start.1 = (f32[512,512]{1,0:T(8,128)S(1)}, f32[512,512]{1,0:T(8,128)}, u32[]{:S(2)}) copy-start(f32[512,512]{1,0:T(8,128)} %param.4) | copy-start | bytes 3145732
  13.6 1.2 %copy-start.3 = (f32[512,512]{1,0:T(8,128)S(1)}, f32[512,512]{1,0:T(8,128)}, u32[]{:S(2)}) copy-start(f32[512,512]{1,0:T(8,128)} %param.7) | copy-start | bytes 3145732
  13.8 1.1 copy-start.2
  16.1 7.7 %collective-permute-start.2 = (f32[64,512]{1,0:T(8,128)S(1)}, f32[64,512]{1,0:T(8,128)S(1)}, u32[]{:S(2)}, u32[]{:S(2)}) collective-permute-start(f32[64,512]{1,0:T(8,128)S(1)} %get-tuple-element.31), channel_id=1, source_target_pairs={{0,1},{1,2},{2,3},{3,4},{4,5},{5,6},{6,7},{7,8},{8,9},{9,10},{10,1... | collective-permute-start | bytes 393224 | tf_op jit(solution)/shard_map/ppermute | solution.py:18
  22.5 3.2 %collective-permute-start.3 = (f32[64,512]{1,0:T(8,128)S(1)}, f32[64,512]{1,0:T(8,128)S(1)}, u32[]{:S(2)}, u32[]{:S(2)}) collective-permute-start(f32[64,512]{1,0:T(8,128)S(1)} %get-tuple-element.30), channel_id=1, source_target_pairs={{1,0},{2,1},{3,2},{4,3},{5,4},{6,5},{7,6},{8,7},{9,8},{10,9},{11,1... | collective-permute-start | bytes 393224 | tf_op jit(solution)/shard_map/ppermute | solution.py:19
  27.0 8.9 %collective-permute-start.4 = (f32[64,512]{1,0:T(8,128)S(1)}, f32[64,512]{1,0:T(8,128)S(1)}, u32[]{:S(2)}, u32[]{:S(2)}) collective-permute-start(f32[64,512]{1,0:T(8,128)S(1)} %get-tuple-element.29), channel_id=1, source_target_pairs={{0,1},{1,2},{2,3},{3,4},{4,5},{5,6},{6,7},{7,8},{8,9},{9,10},{10,1... | collective-permute-start | bytes 393224 | tf_op jit(solution)/shard_map/ppermute | solution.py:18
  34.6 3.2 %collective-permute-start.5 = (f32[64,512]{1,0:T(8,128)S(1)}, f32[64,512]{1,0:T(8,128)S(1)}, u32[]{:S(2)}, u32[]{:S(2)}) collective-permute-start(f32[64,512]{1,0:T(8,128)S(1)} %get-tuple-element.28), channel_id=1, source_target_pairs={{1,0},{2,1},{3,2},{4,3},{5,4},{6,5},{7,6},{8,7},{9,8},{10,9},{11,1... | collective-permute-start | bytes 393224 | tf_op jit(solution)/shard_map/ppermute | solution.py:19
  39.0 9.2 %collective-permute-start.6 = (f32[64,512]{1,0:T(8,128)S(1)}, f32[64,512]{1,0:T(8,128)S(1)}, u32[]{:S(2)}, u32[]{:S(2)}) collective-permute-start(f32[64,512]{1,0:T(8,128)S(1)} %get-tuple-element.27), channel_id=1, source_target_pairs={{0,1},{1,2},{2,3},{3,4},{4,5},{5,6},{6,7},{7,8},{8,9},{9,10},{10,1... | collective-permute-start | bytes 393224 | tf_op jit(solution)/shard_map/ppermute | solution.py:18
  47.0 3.2 %collective-permute-start.7 = (f32[64,512]{1,0:T(8,128)S(1)}, f32[64,512]{1,0:T(8,128)S(1)}, u32[]{:S(2)}, u32[]{:S(2)}) collective-permute-start(f32[64,512]{1,0:T(8,128)S(1)} %get-tuple-element.26), channel_id=1, source_target_pairs={{1,0},{2,1},{3,2},{4,3},{5,4},{6,5},{7,6},{8,7},{9,8},{10,9},{11,1... | collective-permute-start | bytes 393224 | tf_op jit(solution)/shard_map/ppermute | solution.py:19
  51.4 9.1 %collective-permute-start.8 = (f32[64,512]{1,0:T(8,128)S(1)}, f32[64,512]{1,0:T(8,128)S(1)}, u32[]{:S(2)}, u32[]{:S(2)}) collective-permute-start(f32[64,512]{1,0:T(8,128)S(1)} %get-tuple-element.25), channel_id=1, source_target_pairs={{0,1},{1,2},{2,3},{3,4},{4,5},{5,6},{6,7},{7,8},{8,9},{9,10},{10,1... | collective-permute-start | bytes 393224 | tf_op jit(solution)/shard_map/ppermute | solution.py:18
  59.2 3.2 %collective-permute-start.9 = (f32[64,512]{1,0:T(8,128)S(1)}, f32[64,512]{1,0:T(8,128)S(1)}, u32[]{:S(2)}, u32[]{:S(2)}) collective-permute-start(f32[64,512]{1,0:T(8,128)S(1)} %get-tuple-element.24), channel_id=1, source_target_pairs={{1,0},{2,1},{3,2},{4,3},{5,4},{6,5},{7,6},{8,7},{9,8},{10,9},{11,1... | collective-permute-start | bytes 393224 | tf_op jit(solution)/shard_map/ppermute | solution.py:19
  63.6 9.1 %collective-permute-start.10 = (f32[64,512]{1,0:T(8,128)S(1)}, f32[64,512]{1,0:T(8,128)S(1)}, u32[]{:S(2)}, u32[]{:S(2)}) collective-permute-start(f32[64,512]{1,0:T(8,128)S(1)} %get-tuple-element.23), channel_id=1, source_target_pairs={{0,1},{1,2},{2,3},{3,4},{4,5},{5,6},{6,7},{7,8},{8,9},{9,10},{10,1... | collective-permute-start | bytes 393224 | tf_op jit(solution)/shard_map/ppermute | solution.py:18
  71.4 3.2 %collective-permute-start.11 = (f32[64,512]{1,0:T(8,128)S(1)}, f32[64,512]{1,0:T(8,128)S(1)}, u32[]{:S(2)}, u32[]{:S(2)}) collective-permute-start(f32[64,512]{1,0:T(8,128)S(1)} %get-tuple-element.22), channel_id=1, source_target_pairs={{1,0},{2,1},{3,2},{4,3},{5,4},{6,5},{7,6},{8,7},{9,8},{10,9},{11,1... | collective-permute-start | bytes 393224 | tf_op jit(solution)/shard_map/ppermute | solution.py:19
  75.9 9.3 %collective-permute-start.12 = (f32[64,512]{1,0:T(8,128)S(1)}, f32[64,512]{1,0:T(8,128)S(1)}, u32[]{:S(2)}, u32[]{:S(2)}) collective-permute-start(f32[64,512]{1,0:T(8,128)S(1)} %get-tuple-element.21), channel_id=1, source_target_pairs={{0,1},{1,2},{2,3},{3,4},{4,5},{5,6},{6,7},{7,8},{8,9},{9,10},{10,1... | collective-permute-start | bytes 393224 | tf_op jit(solution)/shard_map/ppermute | solution.py:18
  83.8 3.2 %collective-permute-start.13 = (f32[64,512]{1,0:T(8,128)S(1)}, f32[64,512]{1,0:T(8,128)S(1)}, u32[]{:S(2)}, u32[]{:S(2)}) collective-permute-start(f32[64,512]{1,0:T(8,128)S(1)} %get-tuple-element.20), channel_id=1, source_target_pairs={{1,0},{2,1},{3,2},{4,3},{5,4},{6,5},{7,6},{8,7},{9,8},{10,9},{11,1... | collective-permute-start | bytes 393224 | tf_op jit(solution)/shard_map/ppermute | solution.py:19
  88.3 9.1 %collective-permute-start.14 = (f32[64,512]{1,0:T(8,128)S(1)}, f32[64,512]{1,0:T(8,128)S(1)}, u32[]{:S(2)}, u32[]{:S(2)}) collective-permute-start(f32[64,512]{1,0:T(8,128)S(1)} %get-tuple-element.19), channel_id=1, source_target_pairs={{0,1},{1,2},{2,3},{3,4},{4,5},{5,6},{6,7},{7,8},{8,9},{9,10},{10,1... | collective-permute-start | bytes 393224 | tf_op jit(solution)/shard_map/ppermute | solution.py:18
  96.1 3.2 %collective-permute-start.15 = (f32[64,512]{1,0:T(8,128)S(1)}, f32[64,512]{1,0:T(8,128)S(1)}, u32[]{:S(2)}, u32[]{:S(2)}) collective-permute-start(f32[64,512]{1,0:T(8,128)S(1)} %get-tuple-element.18), channel_id=1, source_target_pairs={{1,0},{2,1},{3,2},{4,3},{5,4},{6,5},{7,6},{8,7},{9,8},{10,9},{11,1... | collective-permute-start | bytes 393224 | tf_op jit(solution)/shard_map/ppermute | solution.py:19
